TPU v7x, 32 devices: a whole 2x2x4 slice. The times are simulated.
32 devices in a mesh: row: 8 (over z, core), col: 4 (over y, x).
Axes of the slice: x: 2, y: 2, z: 4, core: 2. Of those that a mesh axis runs over, the one named last changes fastest.
Arguments:
- vectors: bfloat16 [2, 4, 16384], P(None, 'col', 'row'), may hold values from -6 to 6
- lr_left: bfloat16 [8, 4, 32, 8, 2048], P('row', 'col'), may hold values from -0.75 to 0.75
- lr_right: bfloat16 [8, 4, 32, 8, 2048], P('row', 'col'), may hold values from -0.125 to 0.125
- tile_rank: int32 [8, 4, 32], P('row', 'col'), may hold values from 0 to 8, as said below
- leaf_values: bfloat16 [8, 4, 8, 512, 512], P('row', 'col'), may hold values from -0.25 to 0.25
- leaf_places: int32 [8, 4, 8, 2], P('row', 'col'), may hold values from 0 to 31, as said below
- cluster_perm: int32 [8, 8192], P('row'), may hold values from 0 to 65535, as said below
- kappa: float32 [32, 16, 128], P('row', 'col'), may hold values from 0.25 to 4
Outputs:
- prior_action: float32 [2, 32, 16, 128], P(None, 'row', 'col')
Inputs may be any that keep to these rules, and one draw needn't show every extreme that they name: `tile_rank`: 0 exactly on the tiles that contain a leaf, 1 to 8 on the others. `leaf_places`: the 8 leaves of a block are distinct; entry 0 indexes rows and entry 1 column of the block in units of 512. `cluster_perm`: a permutation of all brick indices; within each aligned block of 2048 entries, every value of entry // 2048 occurs exactly 128 times or not at all.
All inputs are finite; a program needn't handle non-finite values.
Results may differ from a plain program's by a relative error of at most 0.0023.
Values may be sent and summed in bfloat16 or wider, within the bound.
A program may use at most 64 MiB of HBM per device.

v0:
```python
import functools

import jax
import jax.numpy as jnp
from jax import lax
from jax.experimental import pallas as pl
from jax.experimental.pallas import tpu as pltpu
from jax.sharding import PartitionSpec as P

CX = 4
CY = 4
TILE_ROWS = 4
TILE_COLS = 8
LANES = 128
MESH = pl.DeviceIdType.MESH
F32 = jnp.float32
BF16 = jnp.bfloat16
NT = (((1,), (1,)), ((), ()))
SIDES = [(a, b) for a in (-1, 0, 1) for b in (-1, 0, 1) if (a, b) != (0, 0)]


def dot_nt(a, b):
    return lax.dot_general(a, b, NT, preferred_element_type=F32)


def pieces(x):
    first = x.astype(BF16).astype(F32)
    rest = x - first
    second = rest.astype(BF16).astype(F32)
    return first, second, rest - second


def iota(shape, dim):
    return lax.broadcasted_iota(jnp.int32, shape, dim)


def kernel(
    rows, cols, kmax, leaf,
    x_hbm, right_hbm, left_hbm, rank_hbm, leaf_hbm, places_hbm, perm_hbm, kappa_hbm,
    out_ref,
    rank_ref, places_ref, near_ref, corner, hc, perm_ref, kappa_ref, right_ref, left_ref, leaf_ref, xg, x32, part, rs, slot_hot,
    msend, rm, vsend, rv, lane_hot, brick, hb, kb, ext, coef, scale,
    local_sem, ag_sem, m_sem, rs_sem, v_sem, k_send, k_recv, h_send, h_recv,
):
    nvec, points = x_hbm.shape
    tile = right_ref.shape[1]
    taps = right_ref.shape[0]
    devices = rows * cols
    nleaf = leaf_ref.shape[0]
    cells = CX * CY
    blocks = points // LANES
    r = lax.axis_index("row")
    c = lax.axis_index("col")
    me = r * cols + c

    own_x = pltpu.make_async_copy(x_hbm, xg.at[r], local_sem.at[3])
    own_perm = pltpu.make_async_copy(
        perm_hbm.at[pl.ds(pl.multiple_of(c * blocks, 8), blocks)], perm_ref, local_sem.at[4]
    )
    own_kappa = pltpu.make_async_copy(kappa_hbm, kappa_ref, local_sem.at[5])
    small = [
        pltpu.make_async_copy(rank_hbm, rank_ref, local_sem.at[6]),
        pltpu.make_async_copy(places_hbm, places_ref, local_sem.at[7]),
    ]
    loads = [
        pltpu.make_async_copy(right_hbm, right_ref, local_sem.at[0]),
        pltpu.make_async_copy(left_hbm, left_ref, local_sem.at[1]),
        pltpu.make_async_copy(leaf_hbm, leaf_ref, local_sem.at[2]),
    ]

    def turned(place, by, count):
        moved = place + by
        return moved - jnp.where(moved >= count, count, 0)

    barrier = pltpu.get_barrier_semaphore()
    for k in range(1, rows):
        pl.semaphore_signal(
            barrier, inc=1, device_id={"row": turned(r, k, rows), "col": c}, device_id_type=MESH
        )
    for k in range(1, cols):
        pl.semaphore_signal(
            barrier, inc=1, device_id={"row": r, "col": turned(c, k, cols)}, device_id_type=MESH
        )
    for load in [own_x, own_perm] + small + [own_kappa] + loads:
        load.start()
    own_x.wait()
    pl.semaphore_wait(barrier, rows + cols - 2)
    for k in range(1, rows):
        pltpu.make_async_remote_copy(
            src_ref=xg.at[r], dst_ref=xg.at[r], send_sem=ag_sem.at[0], recv_sem=ag_sem.at[1],
            device_id={"row": turned(r, k, rows), "col": c}, device_id_type=MESH,
        ).start()

    own_perm.wait()
    targets = perm_ref[...]
    dev_of = targets // points
    place = targets % points
    place_hi = (place // LANES).astype(F32)
    place_lo = (place % LANES).astype(F32)
    dev_ids = iota((devices, LANES), 0)
    hots = [(dev_of[b : b + 1, :] == dev_ids).astype(F32) for b in range(blocks)]
    before = (iota((LANES, LANES), 0) < iota((LANES, LANES), 1)).astype(BF16)
    all_hot = jnp.concatenate(hots, axis=0).astype(BF16)
    inside = jnp.dot(all_hot, before, preferred_element_type=F32)
    totals = jnp.dot(all_hot, jnp.ones((LANES, LANES), BF16), preferred_element_type=F32)
    offset = jnp.zeros((devices, LANES), F32)
    lane_rows = iota((LANES, LANES), 0).astype(F32)
    for b in range(blocks):
        span = slice(b * devices, (b + 1) * devices)
        rank = jnp.sum(hots[b] * (inside[span] + offset), axis=0, keepdims=True)
        offset = offset + totals[span]
        slot_hot[:, b * LANES : (b + 1) * LANES] = (rank == lane_rows).astype(BF16)
    meta = jnp.concatenate(
        [
            jnp.concatenate(
                [hots[b] * place_hi[b : b + 1, :], hots[b] * place_lo[b : b + 1, :]], axis=0
            ).astype(BF16)
            for b in range(blocks)
        ],
        axis=1,
    )
    meta = dot_nt(meta, slot_hot[...])
    for h in range(2):
        msend[:, h, :] = meta[h * devices : (h + 1) * devices]

    for load in small:
        load.wait()
    wide = TILE_COLS * nvec
    lane = iota((1, taps), 1)
    lane_tile, lane_k = lane // kmax, lane % kmax
    ranks = jnp.zeros((1, taps), jnp.int32)
    for t in range(TILE_ROWS * TILE_COLS):
        ranks = jnp.where(lane_tile == t, rank_ref[t], ranks)
    keep = (lane_tile % TILE_COLS == iota((wide, taps), 0) // nvec) & (lane_k < ranks)
    tall = TILE_ROWS * nvec
    fold = (iota((tall, wide), 0) % nvec == iota((tall, wide), 1) % nvec).astype(BF16)
    own_row = lane_tile // TILE_COLS == iota((tall, taps), 0) // nvec
    picks = nleaf * nvec
    row_leaves = cols * points // leaf
    order = iota((1, 3 * picks), 1) % picks
    row_of = jnp.zeros((1, 3 * picks), jnp.int32)
    for l in range(nleaf):
        row_of = jnp.where(order // nvec == l, places_ref[0, l], row_of)
    chosen = iota((row_leaves * nvec, 3 * picks), 0)
    selector = ((chosen // nvec == row_of) & (chosen % nvec == order % nvec)).astype(BF16)

    ext[...] = jnp.zeros_like(ext)
    coef[...] = jnp.zeros_like(coef)
    scale[...] = jnp.zeros_like(scale)

    def exchange(src, dst, sem):
        for dr in range(rows):
            for dc in range(cols):
                if dr + dc:
                    rr, cc = turned(r, dr, rows), turned(c, dc, cols)
                    pltpu.make_async_remote_copy(
                        src_ref=src.at[rr * cols + cc], dst_ref=dst.at[dr * cols + dc - 1],
                        send_sem=sem.at[0], recv_sem=sem.at[1],
                        device_id={"row": rr, "col": cc}, device_id_type=MESH,
                    ).start()
        dst[devices - 1] = src[me]

    def settle(ref, count, sem):
        done = ref.at[pl.ds(0, count)]
        copy = pltpu.make_async_remote_copy(
            src_ref=done, dst_ref=done, send_sem=sem.at[0], recv_sem=sem.at[1],
            device_id={"row": turned(r, 1, rows), "col": c}, device_id_type=MESH,
        )
        return copy

    def side(n):
        dr, dc = SIDES[n]
        rr, cc = r + dr, c + dc
        ok = (rr >= 0) & (rr < rows) & (cc >= 0) & (cc < cols)
        return ok, {"row": jnp.clip(rr, 0, rows - 1), "col": jnp.clip(cc, 0, cols - 1)}

    def side_copy(pick, send, recv, n, incoming):
        slot = n if incoming else len(SIDES) - 1 - n
        src, dst = pick(n, slot)
        return pltpu.make_async_remote_copy(
            src_ref=src, dst_ref=dst, send_sem=send.at[n], recv_sem=recv.at[slot],
            device_id=side(n)[1], device_id_type=MESH,
        )

    def sides_start(pick, send, recv):
        for n in range(len(SIDES)):
            @pl.when(side(n)[0])
            def _():
                side_copy(pick, send, recv, n, False).start()

    def sides_wait(pick, send, recv):
        for n in range(len(SIDES)):
            @pl.when(side(n)[0])
            def _():
                side_copy(pick, send, recv, n, True).wait_recv()
                side_copy(pick, send, recv, n, False).wait_send()

    def kappa_sides(n, slot):
        return kappa_ref, kb.at[slot]

    def field_sides(n, slot):
        if 0 in SIDES[n]:
            return brick, hb.at[slot]
        return corner.at[n], hc.at[slot]

    def corner_cells(dr, dc):
        far_x = [CX - x if dr > 0 else x + 1 for x in range(CX)]
        far_y = [CY - y if dc > 0 else y + 1 for y in range(CY)]
        return [(x, y) for x in range(CX) for y in range(CY) if far_x[x] + far_y[y] <= 4]

    gathered = settle(xg, rows - 1, ag_sem)
    gathered.wait_recv()
    own_kappa.wait()
    sides_start(kappa_sides, k_send, k_recv)
    per = tile // points
    for s in range(rows):
        b, j = s // per, s % per
        x32[nvec * b : nvec * (b + 1), j * points : (j + 1) * points] = xg[s].astype(F32)
    loads[0].wait()
    projected = dot_nt(x32[...].astype(BF16), right_ref[...])
    projected = jnp.where(keep, projected, 0.0).astype(BF16)
    spread_out = jnp.dot(fold, projected, preferred_element_type=F32)
    spread_out = jnp.where(own_row, spread_out, 0.0).astype(BF16)
    loads[1].wait()
    far = jnp.dot(spread_out, left_ref[...], preferred_element_type=F32)
    loads[2].wait()
    subs = points // leaf
    for l in range(nleaf):
        column = places_ref[1, l]
        held = xg[column // subs].astype(F32)
        sub = column % subs
        pick = jnp.zeros((nvec, leaf), F32)
        for q in range(subs):
            pick += jnp.where(sub == q, 1.0, 0.0) * held[:, q * leaf : (q + 1) * leaf]
        near_ref[nvec * l : nvec * (l + 1), :] = dot_nt(pick.astype(BF16), leaf_ref[l])
    near = jnp.concatenate(pieces(near_ref[...]), axis=0).astype(BF16)
    near = jnp.dot(selector, near, preferred_element_type=F32)
    for d in range(cols):
        a, start = d * points // tile, d * points % tile
        for q in range(subs):
            at_row = nvec * (d * subs + q)
            part[d, :, q * leaf : (q + 1) * leaf] = (
                far[nvec * a : nvec * (a + 1), start + q * leaf : start + (q + 1) * leaf]
                + near[at_row : at_row + nvec]
            )
    for k in range(1, cols):
        to = turned(c, k, cols)
        pltpu.make_async_remote_copy(
            src_ref=part.at[to], dst_ref=rs.at[k - 1], send_sem=rs_sem.at[0],
            recv_sem=rs_sem.at[1], device_id={"row": r, "col": to}, device_id_type=MESH,
        ).start()
    exchange(msend, rm, m_sem)

    shares = settle(rs, cols - 1, rs_sem)
    shares.wait_recv()
    action = part[c]
    for k in range(cols - 1):
        action += rs[k]

    terms = pieces(action)
    left_side = jnp.concatenate(
        [
            jnp.concatenate(
                [
                    jnp.where(
                        dev_of[b : b + 1, :] == dev_ids,
                        term[v : v + 1, b * LANES : (b + 1) * LANES],
                        0.0,
                    )
                    for term in terms
                    for v in range(nvec)
                ],
                axis=0,
            ).astype(BF16)
            for b in range(blocks)
        ],
        axis=1,
    )
    packed = dot_nt(left_side, slot_hot[...])
    size = nvec * devices
    packed = packed[:size] + packed[size : 2 * size] + packed[2 * size :]
    for v in range(nvec):
        vsend[:, v, :] = packed[v * devices : (v + 1) * devices]
    exchange(vsend, rv, v_sem)
    sides_wait(kappa_sides, k_send, k_recv)
    strip = 4 * CY

    def laid(ref, get, every):
        for n, (dr, dc) in enumerate(every):
            value = get(dr, dc)
            for x in range(CX):
                at_row = ((dr + 1) * CX + x) * strip + (dc + 1) * CY
                ref[at_row : at_row + CY, :] = value[x * CY : (x + 1) * CY, :]

    every = SIDES + [(0, 0)]

    def valid(dr, dc):
        return (r + dr >= 0) & (r + dr < rows) & (c + dc >= 0) & (c + dc < cols)

    def stiffness(dr, dc):
        if (dr, dc) == (0, 0):
            return (6.0 + kappa_ref[...]) * 0.125
        return jnp.where(valid(dr, dc), (6.0 + kb[SIDES.index((dr, dc))]) * 0.125, 0.0)

    laid(coef, stiffness, every)
    laid(
        scale,
        lambda dr, dc: jnp.full((cells, LANES), jnp.where(valid(dr, dc), 0.125, 0.0), F32),
        every,
    )
    metas = settle(rm, devices - 1, m_sem)
    metas.wait_recv()
    for s in range(devices):
        lane_hot[:, s * LANES : (s + 1) * LANES] = (rm[s, 1:2, :] == lane_rows).astype(BF16)

    values = settle(rv, devices - 1, v_sem)
    values.wait_recv()

    cell_rows = iota((cells, LANES), 0).astype(F32)
    placed = []
    for s in range(devices):
        hit = rm[s, 0:1, :] == cell_rows
        bits = pieces(rv[s])
        placed.append(
            jnp.concatenate(
                [jnp.where(hit, bit[v : v + 1, :], 0.0) for bit in bits for v in range(nvec)],
                axis=0,
            ).astype(BF16)
        )
    field = dot_nt(jnp.concatenate(placed, axis=1), lane_hot[...])
    size = nvec * cells
    field = field[:size] + field[size : 2 * size] + field[2 * size :]
    for v in range(nvec):
        brick[v] = field[v * cells : (v + 1) * cells]
    corners = [n for n in range(len(SIDES)) if 0 not in SIDES[n]]
    for n in corners:
        held = corner_cells(*SIDES[n])
        for v in range(nvec):
            for i, (x, y) in enumerate(held):
                j, cell = v * len(held) + i, v * cells + x * CY + y
                corner[n, j // 4, j % 4 : j % 4 + 1, :] = field[cell : cell + 1]
    sides_start(field_sides, h_send, h_recv)
    gathered.wait_send()
    metas.wait_send()
    shares.wait_send()
    values.wait_send()
    sides_wait(field_sides, h_send, h_recv)

    def bricks(v, dr, dc):
        if (dr, dc) == (0, 0):
            return brick[v]
        return jnp.where(valid(dr, dc), hb[SIDES.index((dr, dc)), v], 0.0)

    for v in range(nvec):
        laid(
            ext.at[v],
            functools.partial(bricks, v),
            [near_side for near_side in every if 0 in near_side],
        )
        for n in corners:
            dr, dc = SIDES[n]
            held = corner_cells(-dr, -dc)
            for i, (x, y) in enumerate(held):
                j = v * len(held) + i
                at_row = ((dr + 1) * CX + x) * strip + (dc + 1) * CY + y
                ext[v, at_row : at_row + 1, :] = jnp.where(
                    valid(dr, dc), hc[n, j // 4, j % 4 : j % 4 + 1, :], 0.0
                )
        cur = ext[v]
        for step in range(4):
            mid = cur[strip:-strip]
            z = iota(mid.shape, 1)
            beside = cur[2 * strip :] + cur[: -2 * strip]
            beside += pltpu.roll(mid, 1, 0) + pltpu.roll(mid, mid.shape[0] - 1, 0)
            beside += jnp.where(z > 0, pltpu.roll(mid, 1, 1), 0.0)
            beside += jnp.where(z < LANES - 1, pltpu.roll(mid, LANES - 1, 1), 0.0)
            low = (step + 1) * strip
            span = slice(low, ext.shape[1] - low)
            cur = coef[span, :] * mid - scale[span, :] * beside
        out_ref[v] = cur.reshape(CX, strip, LANES)


def per_device(
    vectors, lr_left, lr_right, tile_rank, leaf_values, leaf_places, cluster_perm, kappa
):
    rows, cols = lax.axis_size("row"), lax.axis_size("col")
    devices = rows * cols
    nvec, _, points = vectors.shape
    tiles, kmax, tile = lr_left.shape[2:]
    nleaf, leaf = leaf_values.shape[2:4]
    cells, lanes = CX * CY, kappa.shape[2]
    taps = tiles * kmax
    strip, deep = 4 * CY, 3 * CX * 4 * CY
    vmem = pl.BlockSpec(memory_space=pltpu.VMEM)
    hbm = pl.BlockSpec(memory_space=pl.ANY)
    dma = pltpu.SemaphoreType.DMA
    out = pl.pallas_call(
        functools.partial(kernel, rows, cols, kmax, leaf),
        out_shape=pltpu.VMEM((nvec, CX, strip, lanes), F32),
        in_specs=[hbm] * 8,
        out_specs=vmem,
        scratch_shapes=[
            pltpu.SMEM((tiles,), jnp.int32),
            pltpu.SMEM((2, nleaf), jnp.int32),
            pltpu.VMEM((nleaf * nvec, leaf), F32),
            pltpu.VMEM((len(SIDES), 3 * nvec // 2, 4, lanes), F32),
            pltpu.VMEM((len(SIDES), 3 * nvec // 2, 4, lanes), F32),
            pltpu.VMEM((points // LANES, LANES), jnp.int32),
            pltpu.VMEM((cells, lanes), F32),
            pltpu.VMEM((taps, tile), BF16),
            pltpu.VMEM((taps, tile), BF16),
            pltpu.VMEM((nleaf, leaf, leaf), BF16),
            pltpu.VMEM((rows, nvec, points), BF16),
            pltpu.VMEM((TILE_COLS * nvec, tile), F32),
            pltpu.VMEM((cols, nvec, points), F32),
            pltpu.VMEM((cols - 1, nvec, points), F32),
            pltpu.VMEM((LANES, points), BF16),
            pltpu.VMEM((devices, 2, LANES), F32),
            pltpu.VMEM((devices, 2, LANES), F32),
            pltpu.VMEM((devices, nvec, LANES), F32),
            pltpu.VMEM((devices, nvec, LANES), F32),
            pltpu.VMEM((LANES, devices * LANES), BF16),
            pltpu.VMEM((nvec, cells, lanes), F32),
            pltpu.VMEM((len(SIDES), nvec, cells, lanes), F32),
            pltpu.VMEM((len(SIDES), cells, lanes), F32),
            pltpu.VMEM((nvec, deep, lanes), F32),
            pltpu.VMEM((deep, lanes), F32),
            pltpu.VMEM((deep, lanes), F32),
            dma((8,)), dma((2,)), dma((2,)), dma((2,)), dma((2,)),
            dma((len(SIDES),)), dma((len(SIDES),)), dma((len(SIDES),)), dma((len(SIDES),)),
        ],
        compiler_params=pltpu.CompilerParams(collective_id=0, has_side_effects=True),
    )(
        vectors.reshape(nvec, points),
        lr_right.reshape(taps, tile),
        lr_left.reshape(taps, tile),
        tile_rank.reshape(tiles),
        leaf_values.reshape(nleaf, leaf, leaf),
        leaf_places.reshape(nleaf, 2).T,
        cluster_perm.reshape(-1, LANES),
        kappa.reshape(cells, lanes),
    )
    return out[:, :, CY : 2 * CY, :]


def solution(mesh):
    in_specs = (
        P(None, "col", "row"),
        P("row", "col", None, None, None),
        P("row", "col", None, None, None),
        P("row", "col", None),
        P("row", "col", None, None, None),
        P("row", "col", None, None),
        P("row", None),
        P("row", "col", None),
    )
    out_specs = P(None, "row", "col", None)
    return jax.shard_map(
        per_device, mesh=mesh, in_specs=in_specs, out_specs=out_specs, check_vma=False
    )
```

profile of v0, /device:TPU:0, one launch (start us, length us, event | category | flops | bytes accessed | tf_op | source)
XLA Modules:
  0.0 25.4 jit_solution(2068833002073350495)
XLA Ops:
  0.0 24.8 %shard_map.82 = f32[2,4,16,128]{3,2,1,0:T(8,128)S(1)} custom-call(bf16[2,2048]{1,0:T(2,128)(2,1)} %bitcast.14, bf16[256,2048]{1,0:T(8,128)(2,1)} %bitcast.11, bf16[256,2048]{1,0:T(8,128)(2,1)} %bitcast.12, s32[32]{0:T(128)} %bitcast.17, bf16[8,512,512]{2,1,0:T(8,128)(2,1)} %bitcast.10, s32[2,8]{1,0:T(2,128)} %bitcast.16, s32[64,128]{1,0:T(8,128)} %bitcast.13, ...), custom_call_target="tpu_custom_call" | custom-call | tf_op jit(solution)/shard_map/pallas_call | solution.py:397
  24.8 0.6 %slice.3 = f32[2,4,4,128]{3,2,1,0:T(4,128)} slice(f32[2,4,16,128]{3,2,1,0:T(8,128)S(1)} %shard_map.82), slice={[0:2], [0:4], [4:8], [0:128]} | slice | bytes 32768 | tf_op jit(solution)/shard_map/slice | solution.py:443
where the time goes:
time: 25.6 us; the launch traced here: 25.4 us
  Pallas kernels  24.8 us (97%)
  local copies, waits for them, and re-layouts  0.61 us (2%)
    pallas_call x1, Pallas kernels, per_device(): pl.pallas_call(functools.partial(kernel, rows, cols, kmax, leaf), out_sha...  24.8 us
    slice x1, local copies, waits for them, and re-layouts, per_device(): return out[:, :, CY:2 * CY, :]  0.61 us

commit v1 on v0

v1 whole, which is shorter than its diff:
```python
import functools

import jax
import jax.numpy as jnp
from jax import lax
from jax.experimental import pallas as pl
from jax.experimental.pallas import tpu as pltpu
from jax.sharding import PartitionSpec as P

CX = 4
CY = 4
TILE_ROWS = 4
TILE_COLS = 8
LANES = 128
MESH = pl.DeviceIdType.MESH
F32 = jnp.float32
BF16 = jnp.bfloat16
NT = (((1,), (1,)), ((), ()))
SIDES = [(-1, -1), (-1, 1), (1, -1), (1, 1), (0, -1), (0, 1), (-1, 0), (1, 0)]


def dot_nt(a, b):
    return lax.dot_general(a, b, NT, preferred_element_type=F32)


def pieces(x):
    first = x.astype(BF16)
    return first, (x - first.astype(F32)).astype(BF16)


def iota(shape, dim):
    return lax.broadcasted_iota(jnp.int32, shape, dim)


def kernel(
    rows, cols, kmax, leaf,
    x_hbm, right_hbm, left_hbm, rank_hbm, leaf_hbm, places_hbm, perm_hbm, kappa_hbm,
    out_ref,
    rank_ref, places_ref, corner, hc, perm_ref, kappa_ref, right_ref, left_ref, leaf_ref, xg, x32, slot_hot, dest_hot,
    msend, rm, vsend, rv, lane_hot, hit_hot, brick, hb, kb, ext, coef, scale,
    local_sem, ag_sem, m_sem, v_send, v_recv, k_send, k_recv, h_send, h_recv,
):
    subs, nvec = x_hbm.shape[:2]
    points = subs * leaf
    tile = right_ref.shape[1]
    taps = right_ref.shape[0]
    devices = rows * cols
    nleaf = leaf_ref.shape[0]
    cells = CX * CY
    blocks = points // LANES
    r = lax.axis_index("row")
    c = lax.axis_index("col")
    me = r * cols + c

    own_x = pltpu.make_async_copy(x_hbm, xg.at[r], local_sem.at[3])
    own_perm = pltpu.make_async_copy(perm_hbm, perm_ref, local_sem.at[4])
    own_kappa = pltpu.make_async_copy(kappa_hbm, kappa_ref, local_sem.at[5])
    small = [
        pltpu.make_async_copy(rank_hbm, rank_ref, local_sem.at[6]),
        pltpu.make_async_copy(places_hbm, places_ref, local_sem.at[7]),
    ]
    loads = [
        pltpu.make_async_copy(right_hbm, right_ref, local_sem.at[0]),
        pltpu.make_async_copy(left_hbm, left_ref, local_sem.at[1]),
        pltpu.make_async_copy(leaf_hbm, leaf_ref, local_sem.at[2]),
    ]

    def turned(place, by, count):
        moved = place + by
        return moved - jnp.where(moved >= count, count, 0)

    def mirrored(place, by, count):
        if count & (count - 1):
            return turned(place, by, count)
        moved, bit = place, 1
        while bit <= by:
            if by & bit:
                moved = moved + bit - 2 * bit * (place // bit % 2)
            bit *= 2
        return moved

    def far(by):
        return bin(by).count("1")

    row_order = sorted(range(1, rows), key=lambda k: -k)
    col_order = sorted(range(1, cols), key=lambda k: -far(k))
    all_order = sorted(
        ((dr, dc) for dr in range(rows) for dc in range(cols) if dr + dc),
        key=lambda d: -(d[0] // 2 + far(d[1]) + 0.5 * (d[0] % 2)),
    )

    barrier = pltpu.get_barrier_semaphore()
    for k in row_order:
        pl.semaphore_signal(
            barrier, inc=1, device_id={"row": mirrored(r, k, rows), "col": c}, device_id_type=MESH
        )
    for k in col_order:
        pl.semaphore_signal(
            barrier, inc=1, device_id={"row": r, "col": mirrored(c, k, cols)}, device_id_type=MESH
        )
    for load in [own_x, own_perm] + small + [own_kappa] + loads:
        load.start()
    own_x.wait()
    pl.semaphore_wait(barrier, rows + cols - 2)
    for k in row_order:
        pltpu.make_async_remote_copy(
            src_ref=xg.at[r], dst_ref=xg.at[r], send_sem=ag_sem.at[0], recv_sem=ag_sem.at[1],
            device_id={"row": mirrored(r, k, rows), "col": c}, device_id_type=MESH,
        ).start()

    own_perm.wait()
    dev_ids = iota((devices, LANES), 0)
    lane_rows = iota((LANES, LANES), 0).astype(F32)
    ahead = (iota((LANES, 2 * LANES), 0) < iota((LANES, 2 * LANES), 1)).astype(BF16)
    for j in range(cols):
        dev_of = perm_ref[j * blocks : (j + 1) * blocks, :] // points
        hots = [(dev_of[b : b + 1, :] == dev_ids).astype(F32) for b in range(blocks)]
        all_hot = jnp.concatenate(hots, axis=0).astype(BF16)
        counts = jnp.dot(all_hot, ahead, preferred_element_type=F32)
        offset = jnp.zeros((devices, LANES), F32)
        for b in range(blocks):
            span = slice(b * devices, (b + 1) * devices)
            at = (j * blocks + b) * LANES
            rank = jnp.sum(hots[b] * (counts[span, :LANES] + offset), axis=0, keepdims=True)
            offset = offset + counts[span, LANES:]
            slot_hot[:, at : at + LANES] = (rank == lane_rows).astype(BF16)
            dest_hot[:, at : at + LANES] = all_hot[span]
    mine = pl.ds(pl.multiple_of(c * points, LANES), points)
    place = perm_ref[pl.ds(pl.multiple_of(c * blocks, 8), blocks), :] % points
    halves = ((place // LANES).astype(F32), (place % LANES).astype(F32))
    dest_mine = dest_hot[:, mine]
    meta = jnp.concatenate(
        [
            jnp.concatenate(
                [
                    dest_mine[:, b * LANES : (b + 1) * LANES]
                    * jnp.broadcast_to(half[b : b + 1, :], (devices, LANES)).astype(BF16)
                    for b in range(blocks)
                ],
                axis=1,
            )
            for half in halves
        ],
        axis=0,
    )
    meta = dot_nt(meta, slot_hot[:, mine])
    for h in range(2):
        msend[:, h, :] = meta[h * devices : (h + 1) * devices]
    for load in small:
        load.wait()
    wide = TILE_COLS * nvec
    lane = iota((1, taps), 1)
    lane_tile, lane_k = lane // kmax, lane % kmax
    ranks = jnp.zeros((1, taps), jnp.int32)
    for t in range(TILE_ROWS * TILE_COLS):
        ranks = jnp.where(lane_tile == t, rank_ref[t], ranks)
    keep = (lane_tile % TILE_COLS == iota((wide, taps), 0) // nvec) & (lane_k < ranks)
    tall = TILE_ROWS * nvec
    fold = (iota((tall, wide), 0) % nvec == iota((tall, wide), 1) % nvec).astype(BF16)
    own_row = lane_tile // TILE_COLS == iota((tall, taps), 0) // nvec
    row_leaves = cols * points // leaf
    near_rows = iota((row_leaves * nvec, leaf), 0)

    ext[...] = jnp.zeros_like(ext)
    coef[...] = jnp.zeros_like(coef)
    scale[...] = jnp.zeros_like(scale)

    def apart(dr, dc):
        rr, cc = mirrored(r, dr, rows), mirrored(c, dc, cols)
        return rr * cols + cc, {"row": rr, "col": cc}

    def exchange_meta():
        for dr, dc in all_order:
            number, where = apart(dr, dc)
            pltpu.make_async_remote_copy(
                src_ref=msend.at[number], dst_ref=rm.at[dr * cols + c],
                send_sem=m_sem.at[0], recv_sem=m_sem.at[1],
                device_id=where, device_id_type=MESH,
            ).start()
        rm[c] = msend[me]

    def exchange_values():
        for dr, dc in all_order:
            number, where = apart(dr, dc)
            pltpu.make_async_remote_copy(
                src_ref=vsend.at[number], dst_ref=rv.at[dr * cols + dc],
                send_sem=v_send.at[0], recv_sem=v_recv.at[dr],
                device_id=where, device_id_type=MESH,
            ).start()

    def values_of(send, recv, first, count):
        held = rv.at[pl.ds(first, count)]
        return pltpu.make_async_remote_copy(
            src_ref=held, dst_ref=held, send_sem=send, recv_sem=recv,
            device_id={"row": turned(r, 1, rows), "col": c}, device_id_type=MESH,
        )

    def settle(ref, first, count, sem):
        done = ref.at[pl.ds(first, count)]
        copy = pltpu.make_async_remote_copy(
            src_ref=done, dst_ref=done, send_sem=sem.at[0], recv_sem=sem.at[1],
            device_id={"row": turned(r, 1, rows), "col": c}, device_id_type=MESH,
        )
        return copy

    def side(n):
        dr, dc = SIDES[n]
        rr, cc = r + dr, c + dc
        ok = (rr >= 0) & (rr < rows) & (cc >= 0) & (cc < cols)
        return ok, {"row": jnp.clip(rr, 0, rows - 1), "col": jnp.clip(cc, 0, cols - 1)}

    def side_copy(pick, send, recv, n, incoming):
        slot = n if incoming else SIDES.index((-SIDES[n][0], -SIDES[n][1]))
        src, dst = pick(n, slot)
        return pltpu.make_async_remote_copy(
            src_ref=src, dst_ref=dst, send_sem=send.at[n], recv_sem=recv.at[slot],
            device_id=side(n)[1], device_id_type=MESH,
        )

    def sides_start(pick, send, recv):
        for n in range(len(SIDES)):
            @pl.when(side(n)[0])
            def _():
                side_copy(pick, send, recv, n, False).start()

    def sides_wait(pick, send, recv):
        for n in range(len(SIDES)):
            @pl.when(side(n)[0])
            def _():
                side_copy(pick, send, recv, n, True).wait_recv()
                side_copy(pick, send, recv, n, False).wait_send()

    def kappa_sides(n, slot):
        return kappa_ref, kb.at[slot]

    def field_sides(n, slot):
        if 0 in SIDES[n]:
            return brick, hb.at[slot]
        return corner.at[n], hc.at[slot]

    def corner_cells(dr, dc):
        far_x = [CX - x if dr > 0 else x + 1 for x in range(CX)]
        far_y = [CY - y if dc > 0 else y + 1 for y in range(CY)]
        return [(x, y) for x in range(CX) for y in range(CY) if far_x[x] + far_y[y] <= 4]

    gathered = settle(xg, 0, rows - 1, ag_sem)
    gathered.wait_recv()
    for load in loads:
        load.wait()
    own_kappa.wait()
    sides_start(kappa_sides, k_send, k_recv)
    per = tile // points
    for s in range(rows):
        b, j = s // per, s % per
        for q in range(subs):
            at = j * points + q * leaf
            x32[nvec * b : nvec * (b + 1), at : at + leaf] = xg[s, q].astype(F32)
    projected = dot_nt(x32[...].astype(BF16), right_ref[...])
    projected = jnp.where(keep, projected, 0.0).astype(BF16)
    spread_out = jnp.dot(fold, projected, preferred_element_type=F32)
    spread_out = jnp.where(own_row, spread_out, 0.0).astype(BF16)
    exchange_meta()
    far_rows = jnp.dot(spread_out, left_ref[...], preferred_element_type=F32)
    near = jnp.zeros((row_leaves * nvec, leaf), F32)
    for l in range(nleaf):
        column = places_ref[1, l]
        held = xg[column // subs, column % subs].astype(F32)
        spread = jnp.where(near_rows % nvec == 0, held[0:1], held[1:2])
        spread = jnp.where(near_rows // nvec == places_ref[0, l], spread, 0.0)
        near += dot_nt(spread.astype(BF16), leaf_ref[l])
    per_tile = tile // leaf
    for j in range(cols):
        sums = []
        for q in range(subs):
            i = j * subs + q
            at = i % per_tile * leaf
            a = i // per_tile
            sums.append(
                far_rows[nvec * a : nvec * (a + 1), at : at + leaf]
                + near[nvec * i : nvec * (i + 1)]
            )
        terms = pieces(jnp.concatenate(sums, axis=1))
        left_side = jnp.concatenate(
            [
                jnp.concatenate(
                    [
                        dest_hot[:, (j * blocks + b) * LANES : (j * blocks + b + 1) * LANES]
                        * jnp.broadcast_to(
                            term[v : v + 1, b * LANES : (b + 1) * LANES].astype(F32),
                            (devices, LANES),
                        ).astype(BF16)
                        for b in range(blocks)
                    ],
                    axis=1,
                )
                for term in terms
                for v in range(nvec)
            ],
            axis=0,
        )
        packed = dot_nt(left_side, slot_hot[:, j * points : (j + 1) * points])
        packed = packed[: nvec * devices] + packed[nvec * devices :]
        for v in range(nvec):
            vsend[:, j * nvec + v, :] = packed[v * devices : (v + 1) * devices]
    exchange_values()
    sides_wait(kappa_sides, k_send, k_recv)
    strip = 4 * CY

    def laid(ref, get, every):
        for n, (dr, dc) in enumerate(every):
            value = get(dr, dc)
            for x in range(CX):
                at_row = ((dr + 1) * CX + x) * strip + (dc + 1) * CY
                ref[at_row : at_row + CY, :] = value[x * CY : (x + 1) * CY, :]

    every = SIDES + [(0, 0)]

    def valid(dr, dc):
        return (r + dr >= 0) & (r + dr < rows) & (c + dc >= 0) & (c + dc < cols)

    def stiffness(dr, dc):
        if (dr, dc) == (0, 0):
            return (6.0 + kappa_ref[...]) * 0.125
        return jnp.where(valid(dr, dc), (6.0 + kb[SIDES.index((dr, dc))]) * 0.125, 0.0)

    laid(coef, stiffness, every)
    laid(
        scale,
        lambda dr, dc: jnp.full((cells, LANES), jnp.where(valid(dr, dc), 0.125, 0.0), F32),
        every,
    )
    metas = settle(rm, 1, devices - 1, m_sem)
    metas.wait_recv()
    cell_rows = iota((cells, LANES), 0).astype(F32)
    for s in range(devices):
        lane_hot[:, s * LANES : (s + 1) * LANES] = (rm[s, 1:2, :] == lane_rows).astype(BF16)
        hit_hot[:, s * LANES : (s + 1) * LANES] = (rm[s, 0:1, :] == cell_rows).astype(BF16)
    field = jnp.zeros((2 * nvec * cells, LANES), F32)
    for dr in range(rows):
        first = 0 if dr else 1
        values_of(v_send.at[0], v_recv.at[dr], dr * cols + first, cols - first).wait_recv()
        total = rv[dr * cols] if dr else vsend[me]
        for dc in range(1, cols):
            total = total + rv[dr * cols + dc]
        placed = [
            jnp.concatenate(
                [
                    hit_hot[:, (dr * cols + j) * LANES : (dr * cols + j + 1) * LANES]
                    * jnp.broadcast_to(
                        term[j * nvec + v : j * nvec + v + 1, :].astype(F32), (cells, LANES)
                    ).astype(BF16)
                    for j in range(cols)
                ],
                axis=1,
            )
            for term in pieces(total)
            for v in range(nvec)
        ]
        span = slice(dr * cols * LANES, (dr + 1) * cols * LANES)
        field += dot_nt(jnp.concatenate(placed, axis=0), lane_hot[:, span])
    field = field[: nvec * cells] + field[nvec * cells :]
    for v in range(nvec):
        brick[v] = field[v * cells : (v + 1) * cells]
    corners = [n for n in range(len(SIDES)) if 0 not in SIDES[n]]
    for n in corners:
        held = corner_cells(*SIDES[n])
        for v in range(nvec):
            for i, (x, y) in enumerate(held):
                j, cell = v * len(held) + i, v * cells + x * CY + y
                corner[n, j // 4, j % 4 : j % 4 + 1, :] = field[cell : cell + 1]
    sides_start(field_sides, h_send, h_recv)
    gathered.wait_send()
    metas.wait_send()
    values_of(v_send.at[0], v_recv.at[0], 1, devices - 1).wait_send()
    sides_wait(field_sides, h_send, h_recv)

    def bricks(v, dr, dc):
        if (dr, dc) == (0, 0):
            return brick[v]
        return jnp.where(valid(dr, dc), hb[SIDES.index((dr, dc)), v], 0.0)

    for v in range(nvec):
        laid(
            ext.at[v],
            functools.partial(bricks, v),
            [near_side for near_side in every if 0 in near_side],
        )
        for n in corners:
            dr, dc = SIDES[n]
            held = corner_cells(-dr, -dc)
            for i, (x, y) in enumerate(held):
                j = v * len(held) + i
                at_row = ((dr + 1) * CX + x) * strip + (dc + 1) * CY + y
                ext[v, at_row : at_row + 1, :] = jnp.where(
                    valid(dr, dc), hc[n, j // 4, j % 4 : j % 4 + 1, :], 0.0
                )
        cur = ext[v]
        for step in range(4):
            mid = cur[strip:-strip]
            z = iota(mid.shape, 1)
            beside = cur[2 * strip :] + cur[: -2 * strip]
            beside += pltpu.roll(mid, 1, 0) + pltpu.roll(mid, mid.shape[0] - 1, 0)
            beside += jnp.where(z > 0, pltpu.roll(mid, 1, 1), 0.0)
            beside += jnp.where(z < LANES - 1, pltpu.roll(mid, LANES - 1, 1), 0.0)
            low = (step + 1) * strip
            span = slice(low, ext.shape[1] - low)
            cur = coef[span, :] * mid - scale[span, :] * beside
        out_ref[v] = cur.reshape(CX, strip, LANES)


def per_device(
    vectors, lr_left, lr_right, tile_rank, leaf_values, leaf_places, cluster_perm, kappa
):
    rows, cols = lax.axis_size("row"), lax.axis_size("col")
    devices = rows * cols
    nvec, _, points = vectors.shape
    tiles, kmax, tile = lr_left.shape[2:]
    nleaf, leaf = leaf_values.shape[2:4]
    cells, lanes = CX * CY, kappa.shape[2]
    taps = tiles * kmax
    strip, deep = 4 * CY, 3 * CX * 4 * CY
    vmem = pl.BlockSpec(memory_space=pltpu.VMEM)
    hbm = pl.BlockSpec(memory_space=pl.ANY)
    dma = pltpu.SemaphoreType.DMA
    out = pl.pallas_call(
        functools.partial(kernel, rows, cols, kmax, leaf),
        out_shape=pltpu.VMEM((nvec, CX, strip, lanes), F32),
        in_specs=[hbm] * 8,
        out_specs=vmem,
        scratch_shapes=[
            pltpu.SMEM((tiles,), jnp.int32),
            pltpu.SMEM((2, nleaf), jnp.int32),
            pltpu.VMEM((len(SIDES), 3 * nvec // 2, 4, lanes), F32),
            pltpu.VMEM((len(SIDES), 3 * nvec // 2, 4, lanes), F32),
            pltpu.VMEM((cols * points // LANES, LANES), jnp.int32),
            pltpu.VMEM((cells, lanes), F32),
            pltpu.VMEM((taps, tile), BF16),
            pltpu.VMEM((taps, tile), BF16),
            pltpu.VMEM((nleaf, leaf, leaf), BF16),
            pltpu.VMEM((rows, points // leaf, nvec, leaf), BF16),
            pltpu.VMEM((TILE_COLS * nvec, tile), F32),
            pltpu.VMEM((LANES, cols * points), BF16),
            pltpu.VMEM((devices, cols * points), BF16),
            pltpu.VMEM((devices, 2, LANES), F32),
            pltpu.VMEM((devices, 2, LANES), F32),
            pltpu.VMEM((devices, cols * nvec, LANES), F32),
            pltpu.VMEM((devices, cols * nvec, LANES), F32),
            pltpu.VMEM((LANES, devices * LANES), BF16),
            pltpu.VMEM((cells, devices * LANES), BF16),
            pltpu.VMEM((nvec, cells, lanes), F32),
            pltpu.VMEM((len(SIDES), nvec, cells, lanes), F32),
            pltpu.VMEM((len(SIDES), cells, lanes), F32),
            pltpu.VMEM((nvec, deep, lanes), F32),
            pltpu.VMEM((deep, lanes), F32),
            pltpu.VMEM((deep, lanes), F32),
            dma((8,)), dma((2,)), dma((2,)), dma((1,)), dma((rows,)),
            dma((len(SIDES),)), dma((len(SIDES),)), dma((len(SIDES),)), dma((len(SIDES),)),
        ],
        compiler_params=pltpu.CompilerParams(collective_id=0, has_side_effects=True),
    )(
        vectors.reshape(nvec, points // leaf, leaf).transpose(1, 0, 2),
        lr_right.reshape(taps, tile),
        lr_left.reshape(taps, tile),
        tile_rank.reshape(tiles),
        leaf_values.reshape(nleaf, leaf, leaf),
        leaf_places.reshape(nleaf, 2).T,
        cluster_perm.reshape(-1, LANES),
        kappa.reshape(cells, lanes),
    )
    return out[:, :, CY : 2 * CY, :]


def solution(mesh):
    in_specs = (
        P(None, "col", "row"),
        P("row", "col", None, None, None),
        P("row", "col", None, None, None),
        P("row", "col", None),
        P("row", "col", None, None, None),
        P("row", "col", None, None),
        P("row", None),
        P("row", "col", None),
    )
    out_specs = P(None, "row", "col", None)
    return jax.shard_map(
        per_device, mesh=mesh, in_specs=in_specs, out_specs=out_specs, check_vma=False
    )
```

time: 25.6 us -> 22.7 us (0.89)
  Pallas kernels: 24.8 us -> 21.9 us
    pallas_call x1, Pallas kernels: 24.8 us -> 21.9 us  [per_device(): pl.pallas_call(functools.partial(kernel, rows, cols, kmax, leaf), out_sha...]
where the time goes in v1:
time: 22.7 us; the launch traced here: 22.5 us
  Pallas kernels  21.9 us (96%)
  local copies, waits for them, and re-layouts  0.61 us (3%)
    pallas_call x1, Pallas kernels, per_device(): pl.pallas_call(functools.partial(kernel, rows, cols, kmax, leaf), out_sha...  21.9 us
    slice x1, local copies, waits for them, and re-layouts, per_device(): return out[:, :, CY:2 * CY, :]  0.61 us

profile of v1, /device:TPU:0, one launch (start us, length us, event | category | flops | bytes accessed | tf_op | source)
XLA Modules:
  0.0 22.5 jit_solution(2852625436447454338)
XLA Ops:
  0.0 21.9 %shard_map.82 = f32[2,4,16,128]{3,2,1,0:T(8,128)S(1)} custom-call(bf16[4,2,512]{2,1,0:T(2,128)(2,1)} %bitcast.16, bf16[256,2048]{1,0:T(8,128)(2,1)} %bitcast.13, bf16[256,2048]{1,0:T(8,128)(2,1)} %bitcast.14, s32[32]{0:T(128)} %bitcast.19, bf16[8,512,512]{2,1,0:T(8,128)(2,1)} %bitcast.12, s32[2,8]{1,0:T(2,128)} %bitcast.18, s32[64,128]{1,0:T(8,128)} %bitcast.15, ...), custom_call_target="tpu_custom_call" | custom-call | tf_op jit(solution)/shard_map/pallas_call | solution.py:425
  21.9 0.6 %slice.3 = f32[2,4,4,128]{3,2,1,0:T(4,128)} slice(f32[2,4,16,128]{3,2,1,0:T(8,128)S(1)} %shard_map.82), slice={[0:2], [0:4], [4:8], [0:128]} | slice | bytes 32768 | tf_op jit(solution)/shard_map/slice | solution.py:470

commit v2 on v1

--- a/solution.py
+++ b/solution.py
@@ -38,12 +38,11 @@
     out_ref,
     rank_ref, places_ref, corner, hc, perm_ref, kappa_ref, right_ref, left_ref, leaf_ref, xg, x32, slot_hot, dest_hot,
     msend, rm, vsend, rv, lane_hot, hit_hot, brick, hb, kb, ext, coef, scale,
-    local_sem, ag_sem, m_sem, v_send, v_recv, k_send, k_recv, h_send, h_recv,
+    local_sem, ag_send, ag_recv, m_sem, v_send, v_recv, k_send, k_recv, h_send, h_recv,
 ):
     subs, nvec = x_hbm.shape[:2]
     points = subs * leaf
-    tile = right_ref.shape[1]
-    taps = right_ref.shape[0]
+    tile = right_ref.shape[-1]
     devices = rows * cols
     nleaf = leaf_ref.shape[0]
     cells = CX * CY
@@ -104,7 +103,7 @@
     pl.semaphore_wait(barrier, rows + cols - 2)
     for k in row_order:
         pltpu.make_async_remote_copy(
-            src_ref=xg.at[r], dst_ref=xg.at[r], send_sem=ag_sem.at[0], recv_sem=ag_sem.at[1],
+            src_ref=xg.at[r], dst_ref=xg.at[r], send_sem=ag_send.at[0], recv_sem=ag_recv.at[k],
             device_id={"row": mirrored(r, k, rows), "col": c}, device_id_type=MESH,
         ).start()
 
@@ -148,16 +147,9 @@
         msend[:, h, :] = meta[h * devices : (h + 1) * devices]
     for load in small:
         load.wait()
-    wide = TILE_COLS * nvec
-    lane = iota((1, taps), 1)
-    lane_tile, lane_k = lane // kmax, lane % kmax
-    ranks = jnp.zeros((1, taps), jnp.int32)
-    for t in range(TILE_ROWS * TILE_COLS):
-        ranks = jnp.where(lane_tile == t, rank_ref[t], ranks)
-    keep = (lane_tile % TILE_COLS == iota((wide, taps), 0) // nvec) & (lane_k < ranks)
-    tall = TILE_ROWS * nvec
-    fold = (iota((tall, wide), 0) % nvec == iota((tall, wide), 1) % nvec).astype(BF16)
-    own_row = lane_tile // TILE_COLS == iota((tall, taps), 0) // nvec
+    ext[...] = jnp.zeros_like(ext)
+    coef[...] = jnp.zeros_like(coef)
+    scale[...] = jnp.zeros_like(scale)
     row_leaves = cols * points // leaf
     near_rows = iota((row_leaves * nvec, leaf), 0)
 
@@ -243,31 +235,102 @@
         far_y = [CY - y if dc > 0 else y + 1 for y in range(CY)]
         return [(x, y) for x in range(CX) for y in range(CY) if far_x[x] + far_y[y] <= 4]
 
-    gathered = settle(xg, 0, rows - 1, ag_sem)
-    gathered.wait_recv()
-    for load in loads:
+    for load in loads[:2]:
         load.wait()
+    per = tile // points
+    taps = TILE_ROWS * kmax
+    tall = TILE_ROWS * nvec
+    groups = rows // per
+    stages = [range(groups // 2), range(groups // 2, groups)]
+
+    def columns(g):
+        return mirrored(r // per, g, groups)
+
+    def limits(stage):
+        lane = iota((1, len(stage) * taps), 1)
+        most = jnp.zeros((1, len(stage) * taps), jnp.int32)
+        for i, g in enumerate(stage):
+            for a in range(TILE_ROWS):
+                ours = lane // kmax == i * TILE_ROWS + a
+                most = jnp.where(ours, rank_ref[a * TILE_COLS + columns(g)], most)
+        return lane % kmax < most
+
+    within = [limits(stage) for stage in stages]
+
+    def arrive(stage):
+        for g in stage:
+            for k in range(g * per, (g + 1) * per):
+                if k:
+                    s = mirrored(r, k, rows)
+                    pltpu.make_async_remote_copy(
+                        src_ref=xg.at[s], dst_ref=xg.at[s], send_sem=ag_send.at[0],
+                        recv_sem=ag_recv.at[k], device_id={"row": s, "col": c},
+                        device_id_type=MESH,
+                    ).wait_recv()
+
+    def project(stage, kept):
+        high = len(stage) * nvec
+        for g in stage:
+            for j in range(per):
+                for q in range(subs):
+                    at = j * points + q * leaf
+                    x32[nvec * g : nvec * (g + 1), at : at + leaf] = xg[
+                        columns(g) * per + j, q
+                    ].astype(F32)
+        right = jnp.concatenate(
+            [right_ref[:, columns(g)].reshape(taps, tile) for g in stage], axis=0
+        )
+        x_rows = x32[nvec * stage[0] : nvec * (stage[-1] + 1), :].astype(BF16)
+        seen = dot_nt(x_rows, right)
+        row, lane = iota(seen.shape, 0), iota(seen.shape, 1)
+        seen = jnp.where((row // nvec == lane // taps) & kept, seen, 0.0)
+        part, lane = iota((tall, seen.shape[1]), 0), iota((tall, seen.shape[1]), 1)
+        spread = jnp.zeros(part.shape, F32)
+        for v in range(nvec):
+            ours = jnp.sum(jnp.where(row % nvec == v, seen, 0.0), axis=0, keepdims=True)
+            spread = jnp.where(part % nvec == v, ours, spread)
+        spread = jnp.where(lane % taps // kmax == part // nvec, spread, 0.0)
+        return spread.astype(BF16)
+
+    def expand(stage, spread):
+        left = jnp.concatenate(
+            [left_ref[:, columns(g)].reshape(taps, tile) for g in stage], axis=0
+        )
+        return jnp.dot(spread, left, preferred_element_type=F32)
+
+    arrive(stages[0])
+    far_rows = expand(stages[0], project(stages[0], within[0]))
+    loads[2].wait()
     own_kappa.wait()
+    arrive(stages[1])
+    exchange_meta()
     sides_start(kappa_sides, k_send, k_recv)
-    per = tile // points
-    for s in range(rows):
-        b, j = s // per, s % per
-        for q in range(subs):
-            at = j * points + q * leaf
-            x32[nvec * b : nvec * (b + 1), at : at + leaf] = xg[s, q].astype(F32)
-    projected = dot_nt(x32[...].astype(BF16), right_ref[...])
-    projected = jnp.where(keep, projected, 0.0).astype(BF16)
-    spread_out = jnp.dot(fold, projected, preferred_element_type=F32)
-    spread_out = jnp.where(own_row, spread_out, 0.0).astype(BF16)
-    exchange_meta()
-    far_rows = jnp.dot(spread_out, left_ref[...], preferred_element_type=F32)
-    near = jnp.zeros((row_leaves * nvec, leaf), F32)
-    for l in range(nleaf):
+    late = project(stages[1], within[1])
+    halves = 2
+    side_len = leaf // halves
+    straight = [jnp.zeros((row_leaves * nvec, side_len), F32) for _ in range(halves)]
+    turned_near = [jnp.zeros((side_len, row_leaves * nvec), F32) for _ in range(halves)]
+
+    def picked(l):
         column = places_ref[1, l]
         held = xg[column // subs, column % subs].astype(F32)
         spread = jnp.where(near_rows % nvec == 0, held[0:1], held[1:2])
-        spread = jnp.where(near_rows // nvec == places_ref[0, l], spread, 0.0)
-        near += dot_nt(spread.astype(BF16), leaf_ref[l])
+        return jnp.where(near_rows // nvec == places_ref[0, l], spread, 0.0).astype(BF16)
+
+    for l in range(0, nleaf, 2):
+        flat, tall_x = picked(l), picked(l + 1)
+        for k in range(halves):
+            deep = slice(k * side_len, (k + 1) * side_len)
+            for h in range(halves):
+                wide = slice(h * side_len, (h + 1) * side_len)
+                turned_near[h] += dot_nt(leaf_ref[l, wide, deep], flat[:, deep])
+            for h in range(halves):
+                wide = slice(h * side_len, (h + 1) * side_len)
+                straight[h] += dot_nt(tall_x[:, deep], leaf_ref[l + 1, wide, deep])
+        if l == nleaf // 2:
+            far_rows += expand(stages[1], late)
+    near = jnp.concatenate(straight, axis=1)
+    near += jnp.concatenate(turned_near, axis=0).T
     per_tile = tile // leaf
     for j in range(cols):
         sums = []
@@ -369,7 +432,11 @@
                 j, cell = v * len(held) + i, v * cells + x * CY + y
                 corner[n, j // 4, j % 4 : j % 4 + 1, :] = field[cell : cell + 1]
     sides_start(field_sides, h_send, h_recv)
-    gathered.wait_send()
+    rest = xg.at[pl.ds(0, rows - 1)]
+    pltpu.make_async_remote_copy(
+        src_ref=rest, dst_ref=rest, send_sem=ag_send.at[0], recv_sem=ag_recv.at[0],
+        device_id={"row": mirrored(r, 1, rows), "col": c}, device_id_type=MESH,
+    ).wait_send()
     metas.wait_send()
     values_of(v_send.at[0], v_recv.at[0], 1, devices - 1).wait_send()
     sides_wait(field_sides, h_send, h_recv)
@@ -417,7 +484,6 @@
     tiles, kmax, tile = lr_left.shape[2:]
     nleaf, leaf = leaf_values.shape[2:4]
     cells, lanes = CX * CY, kappa.shape[2]
-    taps = tiles * kmax
     strip, deep = 4 * CY, 3 * CX * 4 * CY
     vmem = pl.BlockSpec(memory_space=pltpu.VMEM)
     hbm = pl.BlockSpec(memory_space=pl.ANY)
@@ -434,8 +500,8 @@
             pltpu.VMEM((len(SIDES), 3 * nvec // 2, 4, lanes), F32),
             pltpu.VMEM((cols * points // LANES, LANES), jnp.int32),
             pltpu.VMEM((cells, lanes), F32),
-            pltpu.VMEM((taps, tile), BF16),
-            pltpu.VMEM((taps, tile), BF16),
+            pltpu.VMEM((TILE_ROWS, TILE_COLS, kmax, tile), BF16),
+            pltpu.VMEM((TILE_ROWS, TILE_COLS, kmax, tile), BF16),
             pltpu.VMEM((nleaf, leaf, leaf), BF16),
             pltpu.VMEM((rows, points // leaf, nvec, leaf), BF16),
             pltpu.VMEM((TILE_COLS * nvec, tile), F32),
@@ -453,14 +519,14 @@
             pltpu.VMEM((nvec, deep, lanes), F32),
             pltpu.VMEM((deep, lanes), F32),
             pltpu.VMEM((deep, lanes), F32),
-            dma((8,)), dma((2,)), dma((2,)), dma((1,)), dma((rows,)),
+            dma((8,)), dma((1,)), dma((rows,)), dma((2,)), dma((1,)), dma((rows,)),
             dma((len(SIDES),)), dma((len(SIDES),)), dma((len(SIDES),)), dma((len(SIDES),)),
         ],
         compiler_params=pltpu.CompilerParams(collective_id=0, has_side_effects=True),
     )(
         vectors.reshape(nvec, points // leaf, leaf).transpose(1, 0, 2),
-        lr_right.reshape(taps, tile),
-        lr_left.reshape(taps, tile),
+        lr_right.reshape(TILE_ROWS, TILE_COLS, kmax, tile),
+        lr_left.reshape(TILE_ROWS, TILE_COLS, kmax, tile),
         tile_rank.reshape(tiles),
         leaf_values.reshape(nleaf, leaf, leaf),
         leaf_places.reshape(nleaf, 2).T,

time: 22.7 us -> 22 us (0.969)
  Pallas kernels: 21.9 us -> 21.2 us
    pallas_call x1, Pallas kernels: 21.9 us -> 21.2 us  [per_device(): pl.pallas_call(functools.partial(kernel, rows, cols, kmax, leaf), out_sha...]
where the time goes in v2:
time: 22 us; the launch traced here: 21.8 us
  Pallas kernels  21.2 us (96%)
  local copies, waits for them, and re-layouts  0.61 us (3%)
    pallas_call x1, Pallas kernels, per_device(): pl.pallas_call(functools.partial(kernel, rows, cols, kmax, leaf), out_sha...  21.2 us
    slice x1, local copies, waits for them, and re-layouts, per_device(): return out[:, :, CY:2 * CY, :]  0.61 us

profile of v2, /device:TPU:0, one launch (start us, length us, event | category | flops | bytes accessed | tf_op | source)
XLA Modules:
  0.0 21.8 jit_solution(6248253264815097578)
XLA Ops:
  0.0 21.2 %shard_map.82 = f32[2,4,16,128]{3,2,1,0:T(8,128)S(1)} custom-call(bf16[4,2,512]{2,1,0:T(2,128)(2,1)} %bitcast.16, bf16[4,8,8,2048]{3,2,1,0:T(8,128)(2,1)} %bitcast.13, bf16[4,8,8,2048]{3,2,1,0:T(8,128)(2,1)} %bitcast.14, s32[32]{0:T(128)} %bitcast.19, bf16[8,512,512]{2,1,0:T(8,128)(2,1)} %bitcast.12, s32[2,8]{1,0:T(2,128)} %bitcast.18, s32[64,128]{1,0:T(8,128)} %bitcast.15, ...), custom_call_target="tpu_custom_call" | custom-call | tf_op jit(solution)/shard_map/pallas_call | solution.py:491
  21.2 0.6 %slice.3 = f32[2,4,4,128]{3,2,1,0:T(4,128)} slice(f32[2,4,16,128]{3,2,1,0:T(8,128)S(1)} %shard_map.82), slice={[0:2], [0:4], [4:8], [0:128]} | slice | bytes 32768 | tf_op jit(solution)/shard_map/slice | solution.py:536

commit v3 on v2

--- a/solution.py
+++ b/solution.py
@@ -37,7 +37,7 @@
     x_hbm, right_hbm, left_hbm, rank_hbm, leaf_hbm, places_hbm, perm_hbm, kappa_hbm,
     out_ref,
     rank_ref, places_ref, corner, hc, perm_ref, kappa_ref, right_ref, left_ref, leaf_ref, xg, x32, slot_hot, dest_hot,
-    msend, rm, vsend, rv, lane_hot, hit_hot, brick, hb, kb, ext, coef, scale,
+    msend, rm, vsend, rv, lane_hot, hit_hot, brick, hb, kb, ext, work, coef, scale,
     local_sem, ag_send, ag_recv, m_sem, v_send, v_recv, k_send, k_recv, h_send, h_recv,
 ):
     subs, nvec = x_hbm.shape[:2]
@@ -161,15 +161,14 @@
         rr, cc = mirrored(r, dr, rows), mirrored(c, dc, cols)
         return rr * cols + cc, {"row": rr, "col": cc}
 
-    def exchange_meta():
-        for dr, dc in all_order:
+    def send_meta(peers):
+        for dr, dc in peers:
             number, where = apart(dr, dc)
             pltpu.make_async_remote_copy(
                 src_ref=msend.at[number], dst_ref=rm.at[dr * cols + c],
                 send_sem=m_sem.at[0], recv_sem=m_sem.at[1],
                 device_id=where, device_id_type=MESH,
             ).start()
-        rm[c] = msend[me]
 
     def exchange_values():
         for dr, dc in all_order:
@@ -299,16 +298,18 @@
         return jnp.dot(spread, left, preferred_element_type=F32)
 
     arrive(stages[0])
+    met = len(stages[0]) * per
+    send_meta([d for d in all_order if d[0] < met])
+    rm[c] = msend[me]
     far_rows = expand(stages[0], project(stages[0], within[0]))
     loads[2].wait()
     own_kappa.wait()
     arrive(stages[1])
-    exchange_meta()
-    sides_start(kappa_sides, k_send, k_recv)
+    later = [d for d in all_order if d[0] >= met]
     late = project(stages[1], within[1])
     halves = 2
     side_len = leaf // halves
-    straight = [jnp.zeros((row_leaves * nvec, side_len), F32) for _ in range(halves)]
+    straight = [jnp.zeros((row_leaves * nvec, leaf), F32) for _ in range(halves)]
     turned_near = [jnp.zeros((side_len, row_leaves * nvec), F32) for _ in range(halves)]
 
     def picked(l):
@@ -317,19 +318,31 @@
         spread = jnp.where(near_rows % nvec == 0, held[0:1], held[1:2])
         return jnp.where(near_rows // nvec == places_ref[0, l], spread, 0.0).astype(BF16)
 
+    cuts = [slice(h * side_len, (h + 1) * side_len) for h in range(halves)]
     for l in range(0, nleaf, 2):
         flat, tall_x = picked(l), picked(l + 1)
-        for k in range(halves):
-            deep = slice(k * side_len, (k + 1) * side_len)
-            for h in range(halves):
-                wide = slice(h * side_len, (h + 1) * side_len)
-                turned_near[h] += dot_nt(leaf_ref[l, wide, deep], flat[:, deep])
-            for h in range(halves):
-                wide = slice(h * side_len, (h + 1) * side_len)
-                straight[h] += dot_nt(tall_x[:, deep], leaf_ref[l + 1, wide, deep])
+        turned_near[0] += dot_nt(leaf_ref[l, cuts[0], cuts[0]], flat[:, cuts[0]])
+        send_meta(later[:2])
+        later = later[2:]
+        turned_near[1] += dot_nt(leaf_ref[l, cuts[1], cuts[0]], flat[:, cuts[0]])
+        send_meta(later[:2])
+        later = later[2:]
+        straight[0] += dot_nt(tall_x[:, cuts[0]], leaf_ref[l + 1, :, cuts[0]])
+        send_meta(later[:2])
+        later = later[2:]
+        turned_near[0] += dot_nt(leaf_ref[l, cuts[0], cuts[1]], flat[:, cuts[1]])
+        send_meta(later[:2])
+        later = later[2:]
+        turned_near[1] += dot_nt(leaf_ref[l, cuts[1], cuts[1]], flat[:, cuts[1]])
+        send_meta(later[:2])
+        later = later[2:]
+        straight[1] += dot_nt(tall_x[:, cuts[1]], leaf_ref[l + 1, :, cuts[1]])
+        send_meta(later[:2])
+        later = later[2:]
         if l == nleaf // 2:
             far_rows += expand(stages[1], late)
-    near = jnp.concatenate(straight, axis=1)
+    near = straight[0] + straight[1]
+    send_meta(later)
     near += jnp.concatenate(turned_near, axis=0).T
     per_tile = tile // leaf
     for j in range(cols):
@@ -366,32 +379,7 @@
         for v in range(nvec):
             vsend[:, j * nvec + v, :] = packed[v * devices : (v + 1) * devices]
     exchange_values()
-    sides_wait(kappa_sides, k_send, k_recv)
-    strip = 4 * CY
-
-    def laid(ref, get, every):
-        for n, (dr, dc) in enumerate(every):
-            value = get(dr, dc)
-            for x in range(CX):
-                at_row = ((dr + 1) * CX + x) * strip + (dc + 1) * CY
-                ref[at_row : at_row + CY, :] = value[x * CY : (x + 1) * CY, :]
-
-    every = SIDES + [(0, 0)]
-
-    def valid(dr, dc):
-        return (r + dr >= 0) & (r + dr < rows) & (c + dc >= 0) & (c + dc < cols)
-
-    def stiffness(dr, dc):
-        if (dr, dc) == (0, 0):
-            return (6.0 + kappa_ref[...]) * 0.125
-        return jnp.where(valid(dr, dc), (6.0 + kb[SIDES.index((dr, dc))]) * 0.125, 0.0)
-
-    laid(coef, stiffness, every)
-    laid(
-        scale,
-        lambda dr, dc: jnp.full((cells, LANES), jnp.where(valid(dr, dc), 0.125, 0.0), F32),
-        every,
-    )
+    sides_start(kappa_sides, k_send, k_recv)
     metas = settle(rm, 1, devices - 1, m_sem)
     metas.wait_recv()
     cell_rows = iota((cells, LANES), 0).astype(F32)
@@ -439,6 +427,32 @@
     ).wait_send()
     metas.wait_send()
     values_of(v_send.at[0], v_recv.at[0], 1, devices - 1).wait_send()
+    sides_wait(kappa_sides, k_send, k_recv)
+    strip = 4 * CY
+
+    def laid(ref, get, every):
+        for n, (dr, dc) in enumerate(every):
+            value = get(dr, dc)
+            for x in range(CX):
+                at_row = ((dr + 1) * CX + x) * strip + (dc + 1) * CY
+                ref[at_row : at_row + CY, :] = value[x * CY : (x + 1) * CY, :]
+
+    every = SIDES + [(0, 0)]
+
+    def valid(dr, dc):
+        return (r + dr >= 0) & (r + dr < rows) & (c + dc >= 0) & (c + dc < cols)
+
+    def stiffness(dr, dc):
+        if (dr, dc) == (0, 0):
+            return (6.0 + kappa_ref[...]) * 0.125
+        return jnp.where(valid(dr, dc), (6.0 + kb[SIDES.index((dr, dc))]) * 0.125, 0.0)
+
+    laid(coef, stiffness, every)
+    laid(
+        scale,
+        lambda dr, dc: jnp.full((cells, LANES), jnp.where(valid(dr, dc), 0.125, 0.0), F32),
+        every,
+    )
     sides_wait(field_sides, h_send, h_recv)
 
     def bricks(v, dr, dc):
@@ -461,18 +475,29 @@
                 ext[v, at_row : at_row + 1, :] = jnp.where(
                     valid(dr, dc), hc[n, j // 4, j % 4 : j % 4 + 1, :], 0.0
                 )
-        cur = ext[v]
-        for step in range(4):
-            mid = cur[strip:-strip]
+    rows_in = ext.shape[1]
+    for step in range(4):
+        low = (step + 1) * strip
+        count = rows_in - 2 * low
+        for v in range(nvec):
+            src = ext if step % 2 == 0 else work
+
+            def at(by):
+                return src[v, pl.ds(low + by, count), :]
+
+            mid = src[v, low : low + count, :]
             z = iota(mid.shape, 1)
-            beside = cur[2 * strip :] + cur[: -2 * strip]
-            beside += pltpu.roll(mid, 1, 0) + pltpu.roll(mid, mid.shape[0] - 1, 0)
+            beside = src[v, low + strip : low + strip + count, :]
+            beside += src[v, low - strip : low - strip + count, :]
+            beside += at(1) + at(-1)
             beside += jnp.where(z > 0, pltpu.roll(mid, 1, 1), 0.0)
             beside += jnp.where(z < LANES - 1, pltpu.roll(mid, LANES - 1, 1), 0.0)
-            low = (step + 1) * strip
-            span = slice(low, ext.shape[1] - low)
+            span = slice(low, low + count)
             cur = coef[span, :] * mid - scale[span, :] * beside
-        out_ref[v] = cur.reshape(CX, strip, LANES)
+            if step < 3:
+                (work if step % 2 == 0 else ext)[v, span, :] = cur
+            else:
+                out_ref[v] = cur.reshape(CX, strip, LANES)
 
 
 def per_device(
@@ -517,6 +542,7 @@
             pltpu.VMEM((len(SIDES), nvec, cells, lanes), F32),
             pltpu.VMEM((len(SIDES), cells, lanes), F32),
             pltpu.VMEM((nvec, deep, lanes), F32),
+            pltpu.VMEM((nvec, deep, lanes), F32),
             pltpu.VMEM((deep, lanes), F32),
             pltpu.VMEM((deep, lanes), F32),
             dma((8,)), dma((1,)), dma((rows,)), dma((2,)), dma((1,)), dma((rows,)),

time: 22 us -> 21.6 us (0.982)
  Pallas kernels: 21.2 us -> 20.8 us
    pallas_call x1, Pallas kernels: 21.2 us -> 20.8 us  [per_device(): pl.pallas_call(functools.partial(kernel, rows, cols, kmax, leaf), out_sha...]
where the time goes in v3:
time: 21.6 us; the launch traced here: 21.4 us
  Pallas kernels  20.8 us (96%)
  local copies, waits for them, and re-layouts  0.61 us (3%)
    pallas_call x1, Pallas kernels, per_device(): pl.pallas_call(functools.partial(kernel, rows, cols, kmax, leaf), out_sha...  20.8 us
    slice x1, local copies, waits for them, and re-layouts, per_device(): return out[:, :, CY:2 * CY, :]  0.61 us

profile of v3, /device:TPU:0, one launch (start us, length us, event | category | flops | bytes accessed | tf_op | source)
XLA Modules:
  0.0 21.4 jit_solution(8126812233475754668)
XLA Ops:
  0.0 20.8 %shard_map.82 = f32[2,4,16,128]{3,2,1,0:T(8,128)S(1)} custom-call(bf16[4,2,512]{2,1,0:T(2,128)(2,1)} %bitcast.16, bf16[4,8,8,2048]{3,2,1,0:T(8,128)(2,1)} %bitcast.13, bf16[4,8,8,2048]{3,2,1,0:T(8,128)(2,1)} %bitcast.14, s32[32]{0:T(128)} %bitcast.19, bf16[8,512,512]{2,1,0:T(8,128)(2,1)} %bitcast.12, s32[2,8]{1,0:T(2,128)} %bitcast.18, s32[64,128]{1,0:T(8,128)} %bitcast.15, ...), custom_call_target="tpu_custom_call" | custom-call | tf_op jit(solution)/shard_map/pallas_call | solution.py:516
  20.8 0.6 %slice.3 = f32[2,4,4,128]{3,2,1,0:T(4,128)} slice(f32[2,4,16,128]{3,2,1,0:T(8,128)S(1)} %shard_map.82), slice={[0:2], [0:4], [4:8], [0:128]} | slice | bytes 32768 | tf_op jit(solution)/shard_map/slice | solution.py:562

commit v4 on v3

--- a/solution.py
+++ b/solution.py
@@ -26,6 +26,24 @@
 def pieces(x):
     first = x.astype(BF16)
     return first, (x - first.astype(F32)).astype(BF16)
+
+
+def span_of(grade):
+    return jnp.exp2(grade.astype(F32) * 0.125)
+
+
+def coded(values, grade):
+    first, second = (
+        jnp.floor(v * (32000.0 / span_of(grade)) + 0.5).astype(jnp.int32) for v in values
+    )
+    return first * 65536 + second
+
+
+def decoded(code, grade):
+    second = jnp.right_shift(jnp.left_shift(code, 16), 16)
+    first = jnp.right_shift(code - second, 16)
+    unit = span_of(grade) * (1.0 / 32000.0)
+    return first.astype(F32) * unit, second.astype(F32) * unit
 
 
 def iota(shape, dim):
@@ -174,13 +192,14 @@
         for dr, dc in all_order:
             number, where = apart(dr, dc)
             pltpu.make_async_remote_copy(
-                src_ref=vsend.at[number], dst_ref=rv.at[dr * cols + dc],
+                src_ref=vsend.at[number, pl.ds(0, cols + 1)],
+                dst_ref=rv.at[dr * cols + dc, pl.ds(0, cols + 1)],
                 send_sem=v_send.at[0], recv_sem=v_recv.at[dr],
                 device_id=where, device_id_type=MESH,
             ).start()
 
     def values_of(send, recv, first, count):
-        held = rv.at[pl.ds(first, count)]
+        held = rv.at[pl.ds(first, count), pl.ds(0, cols + 1)]
         return pltpu.make_async_remote_copy(
             src_ref=held, dst_ref=held, send_sem=send, recv_sem=recv,
             device_id={"row": turned(r, 1, rows), "col": c}, device_id_type=MESH,
@@ -345,6 +364,7 @@
     send_meta(later)
     near += jnp.concatenate(turned_near, axis=0).T
     per_tile = tile // leaf
+    packs, tops = [], []
     for j in range(cols):
         sums = []
         for q in range(subs):
@@ -355,7 +375,9 @@
                 far_rows[nvec * a : nvec * (a + 1), at : at + leaf]
                 + near[nvec * i : nvec * (i + 1)]
             )
-        terms = pieces(jnp.concatenate(sums, axis=1))
+        sums = jnp.concatenate(sums, axis=1)
+        tops.append(jnp.max(jnp.abs(sums), axis=0, keepdims=True))
+        terms = pieces(sums)
         left_side = jnp.concatenate(
             [
                 jnp.concatenate(
@@ -375,9 +397,15 @@
             axis=0,
         )
         packed = dot_nt(left_side, slot_hot[:, j * points : (j + 1) * points])
-        packed = packed[: nvec * devices] + packed[nvec * devices :]
-        for v in range(nvec):
-            vsend[:, j * nvec + v, :] = packed[v * devices : (v + 1) * devices]
+        packs.append(packed[: nvec * devices] + packed[nvec * devices :])
+    top = jnp.max(functools.reduce(jnp.maximum, tops), axis=1, keepdims=True)
+    grade = jnp.ceil(jnp.log2(jnp.maximum(top, 1e-30)) * 8.0 + 0.01).astype(jnp.int32)
+    grade = jnp.broadcast_to(grade, (devices, LANES))
+    for j in range(cols):
+        vsend[:, j, :] = coded(
+            [packs[j][v * devices : (v + 1) * devices] for v in range(nvec)], grade
+        )
+    vsend[:, cols, :] = grade
     exchange_values()
     sides_start(kappa_sides, k_send, k_recv)
     metas = settle(rm, 1, devices - 1, m_sem)
@@ -390,21 +418,24 @@
     for dr in range(rows):
         first = 0 if dr else 1
         values_of(v_send.at[0], v_recv.at[dr], dr * cols + first, cols - first).wait_recv()
-        total = rv[dr * cols] if dr else vsend[me]
-        for dc in range(1, cols):
-            total = total + rv[dr * cols + dc]
+        totals = [jnp.zeros((cols, LANES), F32) for _ in range(nvec)]
+        for dc in range(cols):
+            held = rv.at[dr * cols + dc] if dr + dc else vsend.at[me]
+            parts = decoded(held[0:cols, :], held[cols : cols + 1, :])
+            totals = [total + part for total, part in zip(totals, parts)]
+        terms = [pieces(total) for total in totals]
         placed = [
             jnp.concatenate(
                 [
                     hit_hot[:, (dr * cols + j) * LANES : (dr * cols + j + 1) * LANES]
                     * jnp.broadcast_to(
-                        term[j * nvec + v : j * nvec + v + 1, :].astype(F32), (cells, LANES)
+                        terms[v][i][j : j + 1, :].astype(F32), (cells, LANES)
                     ).astype(BF16)
                     for j in range(cols)
                 ],
                 axis=1,
             )
-            for term in pieces(total)
+            for i in range(2)
             for v in range(nvec)
         ]
         span = slice(dr * cols * LANES, (dr + 1) * cols * LANES)
@@ -534,8 +565,8 @@
             pltpu.VMEM((devices, cols * points), BF16),
             pltpu.VMEM((devices, 2, LANES), F32),
             pltpu.VMEM((devices, 2, LANES), F32),
-            pltpu.VMEM((devices, cols * nvec, LANES), F32),
-            pltpu.VMEM((devices, cols * nvec, LANES), F32),
+            pltpu.VMEM((devices, cols * nvec, LANES), jnp.int32),
+            pltpu.VMEM((devices, cols * nvec, LANES), jnp.int32),
             pltpu.VMEM((LANES, devices * LANES), BF16),
             pltpu.VMEM((cells, devices * LANES), BF16),
             pltpu.VMEM((nvec, cells, lanes), F32),

time: 21.6 us -> 20.8 us (0.963)
  Pallas kernels: 20.8 us -> 20 us
    pallas_call x1, Pallas kernels: 20.8 us -> 20 us  [per_device(): pl.pallas_call(functools.partial(kernel, rows, cols, kmax, leaf), out_sha...]
where the time goes in v4:
time: 20.8 us; the launch traced here: 20.6 us
  Pallas kernels  20 us (96%)
  local copies, waits for them, and re-layouts  0.61 us (3%)
    pallas_call x1, Pallas kernels, per_device(): pl.pallas_call(functools.partial(kernel, rows, cols, kmax, leaf), out_sha...  20 us
    slice x1, local copies, waits for them, and re-layouts, per_device(): return out[:, :, CY:2 * CY, :]  0.61 us

profile of v4, /device:TPU:0, one launch (start us, length us, event | category | flops | bytes accessed | tf_op | source)
XLA Modules:
  0.0 20.6 jit_solution(5774882456728793374)
XLA Ops:
  0.0 20.0 %shard_map.82 = f32[2,4,16,128]{3,2,1,0:T(8,128)S(1)} custom-call(bf16[4,2,512]{2,1,0:T(2,128)(2,1)} %bitcast.16, bf16[4,8,8,2048]{3,2,1,0:T(8,128)(2,1)} %bitcast.13, bf16[4,8,8,2048]{3,2,1,0:T(8,128)(2,1)} %bitcast.14, s32[32]{0:T(128)} %bitcast.19, bf16[8,512,512]{2,1,0:T(8,128)(2,1)} %bitcast.12, s32[2,8]{1,0:T(2,128)} %bitcast.18, s32[64,128]{1,0:T(8,128)} %bitcast.15, ...), custom_call_target="tpu_custom_call" | custom-call | tf_op jit(solution)/shard_map/pallas_call | solution.py:547
  20.0 0.6 %slice.3 = f32[2,4,4,128]{3,2,1,0:T(4,128)} slice(f32[2,4,16,128]{3,2,1,0:T(8,128)S(1)} %shard_map.82), slice={[0:2], [0:4], [4:8], [0:128]} | slice | bytes 32768 | tf_op jit(solution)/shard_map/slice | solution.py:593

commit v5 on v4

--- a/solution.py
+++ b/solution.py
@@ -16,7 +16,7 @@
 F32 = jnp.float32
 BF16 = jnp.bfloat16
 NT = (((1,), (1,)), ((), ()))
-SIDES = [(-1, -1), (-1, 1), (1, -1), (1, 1), (0, -1), (0, 1), (-1, 0), (1, 0)]
+SIDES = [(0, -1), (0, 1), (-1, -1), (-1, 1), (1, -1), (1, 1), (-1, 0), (1, 0)]
 
 
 def dot_nt(a, b):

time: 20.8 us -> 20.6 us (level)
  no operation moved by 1% of the time
where the time goes in v5:
time: 20.6 us; the launch traced here: 20.5 us
  Pallas kernels  19.8 us (96%)
  local copies, waits for them, and re-layouts  0.61 us (3%)
    pallas_call x1, Pallas kernels, per_device(): pl.pallas_call(functools.partial(kernel, rows, cols, kmax, leaf), out_sha...  19.8 us
    slice x1, local copies, waits for them, and re-layouts, per_device(): return out[:, :, CY:2 * CY, :]  0.61 us

profile of v5, /device:TPU:0, one launch (start us, length us, event | category | flops | bytes accessed | tf_op | source)
XLA Modules:
  0.0 20.5 jit_solution(991125388734682026)
XLA Ops:
  0.0 19.8 %shard_map.82 = f32[2,4,16,128]{3,2,1,0:T(8,128)S(1)} custom-call(bf16[4,2,512]{2,1,0:T(2,128)(2,1)} %bitcast.16, bf16[4,8,8,2048]{3,2,1,0:T(8,128)(2,1)} %bitcast.13, bf16[4,8,8,2048]{3,2,1,0:T(8,128)(2,1)} %bitcast.14, s32[32]{0:T(128)} %bitcast.19, bf16[8,512,512]{2,1,0:T(8,128)(2,1)} %bitcast.12, s32[2,8]{1,0:T(2,128)} %bitcast.18, s32[64,128]{1,0:T(8,128)} %bitcast.15, ...), custom_call_target="tpu_custom_call" | custom-call | tf_op jit(solution)/shard_map/pallas_call | solution.py:547
  19.8 0.6 %slice.3 = f32[2,4,4,128]{3,2,1,0:T(4,128)} slice(f32[2,4,16,128]{3,2,1,0:T(8,128)S(1)} %shard_map.82), slice={[0:2], [0:4], [4:8], [0:128]} | slice | bytes 32768 | tf_op jit(solution)/shard_map/slice | solution.py:593
